TPU v7x, 512 devices: a whole 4x8x8 slice. The times are simulated.
512 devices in a mesh: seed: 2 (over core), dp: 4 (over x), tensor: 64 (over z, y).
Axes of the slice: x: 4, y: 8, z: 8, core: 2. Of those that a mesh axis runs over, the one named last changes fastest.
Arguments:
- hidden: bfloat16 [2, 64, 96, 2048], P('seed', 'dp', None, 'tensor'), may hold values from -24 to 24
- norm_gain: float32 [2, 2048], P('seed'), may hold values from 0.25 to 1.75
- lm_head: bfloat16 [2, 2048, 65536], P('seed', None, 'tensor'), may hold values from -3 to 3
- targets: int32 [64, 96], P('dp'), may hold values from 0 to 65535
- lengths: int32 [64], P('dp'), may hold values from 24 to 96
Outputs:
- token_scores: float32 [2, 64, 96], P('seed', 'dp')
- ensemble: float32 [64], P('dp')
- centered: float32 [64], P('dp')
All inputs are finite; a program needn't handle non-finite values.
Results may differ from a plain program's by a relative error of at most 0.0003.
The roundings to bfloat16 on the way count: a program that leaves them out, or rounds other values in their place, can miss the bound.
Values may be sent and summed in bfloat16 or wider, within the bound.
A program may use at most 128 MiB of HBM per device.

v0:
```python
import jax
import jax.numpy as jnp
from jax import lax
from jax.sharding import Mesh
from jax.sharding import PartitionSpec as P

TENSOR = ("tensor_0", "tensor_1")
rms_epsilon = 1e-05


def gathered_once(x, axis):
    leaves = jax.tree.leaves(x)
    sequence = sorted(range(len(leaves)), key=lambda k: -leaves[k].size)
    width = (1, *leaves[sequence[0]].shape)[-1]
    lines = [
        jnp.pad(leaves[k].reshape(-1), (0, -leaves[k].size % width)).reshape(-1, width)
        for k in sequence
    ]
    both, at, found = (lax.all_gather(jnp.concatenate(lines), axis), 0, {})
    for k, line in zip(sequence, lines):
        piece = both[:, at : at + len(line)].reshape(len(both), -1)
        found[k] = piece[:, : leaves[k].size].reshape(-1, *leaves[k].shape)
        at += len(line)
    numbers = iter(range(len(leaves)))
    return jax.tree.map(lambda _: found[next(numbers)], x)


def joined_all(x, axes, combine):
    for axis in axes:
        pieces = gathered_once(x, axis)
        x = jax.tree.map(lambda part: part[0], pieces)
        for k in range(1, lax.axis_size(axis)):
            x = combine(x, jax.tree.map(lambda part: part[k], pieces))
    return x


def from_everyone(x, axis):
    peers = lax.axis_size(axis)
    return lax.all_to_all(jnp.broadcast_to(x[None], (peers, *x.shape)), axis, 0, 0, tiled=True)


def taken_together(x, axis):
    return from_everyone(x, axis).sum(axis=0)


def combine_parts(first, second):
    top_value = jnp.maximum(first[0], second[0])
    left = jnp.exp(first[0] - top_value)
    right = jnp.exp(second[0] - top_value)
    return (
        top_value,
        first[1] * left + second[1] * right,
        first[2] * left * left + second[2] * right * right,
        first[3] * left + second[3] * right,
    )


def shards(hidden, norm_gain, lm_head, targets, lengths):
    per_group, seq_len, own_width = (hidden.shape[1], hidden.shape[2], hidden.shape[3])
    full_width = norm_gain.shape[1]
    own_vocab = lm_head.shape[2]
    row_count = per_group * seq_len
    weight = lm_head[0]
    gain = norm_gain[0]
    whole = lax.all_gather(hidden, TENSOR, axis=3, tiled=True)
    flat = whole.reshape(row_count, full_width).astype(jnp.float32)
    mean_sq = jnp.mean(flat * flat, axis=1, keepdims=True)
    normed = (flat * lax.rsqrt(mean_sq + rms_epsilon) * gain).astype(jnp.bfloat16)
    logits = jnp.dot(normed, weight, preferred_element_type=jnp.float32)
    first_column = lax.axis_index(TENSOR) * own_vocab
    column = jnp.arange(own_vocab, dtype=jnp.int32) + first_column
    onehot = column[None, :] == targets.reshape(row_count)[:, None]
    local_top = jnp.max(logits, axis=1)
    scaled_exp = jnp.exp(logits - local_top[:, None])
    merged = joined_all(
        (
            local_top,
            jnp.sum(scaled_exp, axis=1),
            jnp.sum(scaled_exp * scaled_exp, axis=1),
            jnp.sum(jnp.where(onehot, scaled_exp, 0.0), axis=1),
        ),
        TENSOR,
        combine_parts,
    )
    exp_mass, exp_square, exp_target = (merged[1], merged[2], merged[3])
    spread = jnp.maximum(
        exp_square / (exp_mass * exp_mass) - 2.0 * exp_target / exp_mass + 1.0, 0.0
    )
    scores = jnp.sqrt(spread).reshape(per_group, seq_len)
    position = jnp.arange(seq_len, dtype=jnp.int32)
    valid = position[None, :] < lengths[:, None]
    token_scores = jnp.where(valid, scores, jnp.float32(0.0))
    example_scores = jnp.sum(token_scores, axis=1) / lengths.astype(jnp.float32)
    members = lax.axis_size("seed")
    groups = lax.axis_size("dp")
    slots = jnp.zeros((groups * per_group,), jnp.float32)
    slots = lax.dynamic_update_slice_in_dim(
        slots, example_scores, lax.axis_index("dp") * per_group, 0
    )
    everyone = taken_together(slots, ("seed", "dp")) / members
    ensemble = lax.dynamic_slice_in_dim(everyone, lax.axis_index("dp") * per_group, per_group, 0)
    centered = ensemble - jnp.sum(everyone) / (per_group * groups)
    return (token_scores[None, :, :], ensemble, centered)


def solution(mesh):
    finer = Mesh(
        mesh.devices.reshape(mesh.shape["seed"], mesh.shape["dp"], 8, 8),
        ("seed", "dp", "tensor_0", "tensor_1"),
    )
    in_specs = (
        P("seed", "dp", None, TENSOR),
        P("seed", None),
        P("seed", None, TENSOR),
        P("dp", None),
        P("dp"),
    )
    out_specs = (P("seed", "dp", None), P("dp"), P("dp"))
    return jax.shard_map(
        shards, mesh=finer, in_specs=in_specs, out_specs=out_specs, check_vma=False
    )
```

profile of v0, /device:TPU:1, one launch (start us, length us, event | category | flops | bytes accessed | tf_op | source)
XLA Modules:
  0.0 219.5 jit_solution(6617547372947440160)
XLA Ops:
  7.2 1.6 copy.13
  8.9 0.8 eq.16
  9.6 105.8 %all-gather.6.cloned.1.call-done = bf16[1,16,96,2048]{2,1,0,3:T(8,128)(2,1)} async-done(((bf16[1,16,96,32]{2,1,0,3:T(8,128)(2,1)}), bf16[1,16,96,2048]{2,1,0,3:T(8,128)(2,1)}) %all-gather.6.cloned.1.call-update) | async-done | bytes 6291472 | tf_op jit(solution)/shard_map/all_gather | solution.py:65
  115.4 11.8 %copy.14 = bf16[1,16,96,2048]{3,2,1,0:T(8,128)(2,1)} copy(bf16[1,16,96,2048]{2,1,0,3:T(8,128)(2,1)} %all-gather.6.cloned.1.call-done) | data formatting | bytes 12582912 | tf_op jit(solution)/shard_map/all_gather | solution.py:65
  127.2 4.2 %fusion = f32[16,96]{1,0:T(8,128)S(1)} fusion(bf16[1,16,96,2048]{3,2,1,0:T(8,128)(2,1)} %copy.14), kind=kLoop, calls=%fused_computation.2 | loop fusion | flops 9435648 | bytes 6297600 | tf_op jit(solution)/shard_map/reduce_sum | solution.py:67
  131.4 0.3 copy-done
  131.8 1.5 fusion.2
  133.3 0.7 copy-done.3
  134.0 7.4 %fusion.103 = (f32[1536]{0:T(1024)S(1)}, f32[1536,1024]{0,1:T(8,128)S(1)}) fusion(bf16[1536,2048]{1,0:T(8,128)(2,1)S(1)} %bitcast.341, bf16[1,2048,1024]{2,1,0:T(8,128)(2,1)S(1)} %copy-done.3), kind=kOutput, calls=%fused_computation.251 | convolution fusion | flops 6444022272 | bytes 16783360 | tf_op jit(solution)/shard_map/dot_general | solution.py:69
  141.4 2.3 %fusion.3 = (f32[1536]{0:T(1024)S(1)}, f32[1536]{0:T(1024)S(1)}, f32[1536]{0:T(1024)S(1)}) fusion(f32[1536,1024]{0,1:T(8,128)S(1)} %get-tuple-element.48, f32[1536]{0:T(1024)S(1)} %get-tuple-element.47, s32[1536]{0:T(1024)S(1)} %eq.16, s32[1024]{0:T(1024)S(1)} %iota_add_fusion), kind=kLoop, calls=%fused_computation.8 | loop fusion | flops 11005440 | bytes 6326272 | tf_op jit(solution)/shard_map/reduce_sum | solution.py:78
  143.8 19.5 %all-gather.2 = f32[8,4,1536]{2,1,0:T(4,128)S(1)} all-gather(f32[1,4,1536]{2,1,0:T(4,128)S(1)} %maximum_bitcast_fusion), channel_id=2, replica_groups=mesh['seed'=2,'dp'=4,'tensor_0'=8,'tensor_1'=8] {'tensor_0'}, dimensions={0}, use_global_device_ids=true | all-gather | bytes 221184 | tf_op jit(solution)/shard_map/all_gather | solution.py:19
  163.4 0.1 fusion.71
  163.5 0.2 fusion.48
  163.7 0.1 fusion.50
  163.9 18.9 %all-gather.3 = f32[8,4,1536]{2,1,0:T(4,128)S(1)} all-gather(f32[1,4,1536]{2,1,0:T(4,128)S(1)} %maximum_bitcast_fusion.1), channel_id=3, replica_groups=mesh['seed'=2,'dp'=4,'tensor_0'=8,'tensor_1'=8] {'tensor_1'}, dimensions={0}, use_global_device_ids=true | all-gather | bytes 221184 | tf_op jit(solution)/shard_map/all_gather | solution.py:19
  182.7 0.3 slice_reduce_fusion.30
  183.0 0.2 slice_reduce_fusion.31
  183.3 0.1 squeeze.325
  186.1 0.1 squeeze.326
  186.2 0.1 squeeze.294
  186.3 0.1 squeeze.327
  186.3 0.1 squeeze.295
  186.4 0.1 squeeze.328
  186.5 0.1 squeeze.296
  187.9 0.2 select_reduce_fusion.1
  188.1 0.1 divide_dynamic-update-slice_fusion
  188.2 0.6 broadcast_in_dim.8
  188.8 17.4 %all-to-all-start = ((f32[8,1,64]{2,1,0:T(1,128)}), f32[8,1,64]{2,1,0:T(1,128)S(1)}, u32[]{:S(2)}, u32[]{:S(2)}) async-start(f32[8,1,64]{2,1,0:T(1,128)} %broadcast_in_dim.8), calls=%async_computation | async-start | bytes 8192 | tf_op jit(solution)/shard_map/all_to_all | solution.py:39
  206.2 0.7 sqrt_select_fusion
  206.9 3.9 %all-to-all-done = f32[8,1,64]{2,1,0:T(1,128)S(1)} async-done(((f32[8,1,64]{2,1,0:T(1,128)}), f32[8,1,64]{2,1,0:T(1,128)S(1)}, u32[]{:S(2)}, u32[]{:S(2)}) %all-to-all-start) | async-done | bytes 2080 | tf_op jit(solution)/shard_map/all_to_all | solution.py:39
  210.8 0.6 broadcast_multiply_fusion
  212.1 0.6 broadcast_subtract_fusion
  (75 shorter events, 4.2 us)
Async XLA Ops:
  7.2 108.2 %all-gather.6.cloned.1.call-start = ((), (), s32[]{:S(2)}) async-start(), calls=%async_computation.1 | async-start | bytes 8519680 | tf_op jit(solution)/shard_map/all_gather | solution.py:65
  127.2 4.6 %copy-start = (bf16[1,16,96,2048]{3,2,1,0:T(8,128)(2,1)S(1)}, bf16[1,16,96,2048]{3,2,1,0:T(8,128)(2,1)}, u32[]{:S(2)}) copy-start(bf16[1,16,96,2048]{3,2,1,0:T(8,128)(2,1)} %copy.14) | copy-start | bytes 18874372
  127.2 4.6 %copy-start.1 = (f32[1,2048]{1,0:T(1,128)S(1)}, f32[1,2048]{1,0:T(1,128)}, u32[]{:S(2)}) copy-start(f32[1,2048]{1,0:T(1,128)} %param.6) | copy-start | bytes 24580
  131.8 2.2 copy-start.3
  141.4 46.5 %copy-start.2 = (s32[16]{0:T(128)S(1)}, s32[16]{0:T(128)}, u32[]{:S(2)}) copy-start(s32[16]{0:T(128)} %param.9) | copy-start | bytes 196
  188.8 22.0 %all-to-all-start = ((f32[8,1,64]{2,1,0:T(1,128)}), f32[8,1,64]{2,1,0:T(1,128)S(1)}, u32[]{:S(2)}, u32[]{:S(2)}) async-start(f32[8,1,64]{2,1,0:T(1,128)} %broadcast_in_dim.8), calls=%async_computation | async-start | bytes 8192 | tf_op jit(solution)/shard_map/all_to_all | solution.py:39
Sparse Core Ops, SparseCore 0:
  11.0 104.3 all-gather.5
where the time goes:
time: 220 us
  waiting for transfers between devices  110 us (50%)
  blocking collectives  38.4 us (17%)
  local copies, waits for them, and re-layouts  20.9 us (10%)
  starting transfers between devices  17.4 us (8%)
  between operations  14.9 us (7%)
  other arithmetic  10.9 us (5%)
  matrix products  7.38 us (3%)
    all_gather x1, waiting for transfers between devices, shards(): whole = lax.all_gather(hidden, TENSOR, axis=3, tiled=True)  106 us
    all_gather x2, blocking collectives, gathered_once(): both, at, found = (lax.all_gather(jnp.concatenate(lines), axis), 0, {})  38.4 us
    all_to_all x1, starting transfers between devices, from_everyone(): lax.all_to_all(jnp.broadcast_to(x[None], (peers, *x.shape)), axis, 0, 0,...  17.4 us
    all_gather x1, local copies, waits for them, and re-layouts, shards(): whole = lax.all_gather(hidden, TENSOR, axis=3, tiled=True)  11.8 us
    dot_general x1, matrix products, shards(): logits = jnp.dot(normed, weight, preferred_element_type=jnp.float32)  7.38 us
  transfers between devices with their start and end apart: 2, of which 2 were waited for; matrix products, arithmetic and copies ran while one was open for 1% of the time, Pallas kernels for 0%

commit v1 on v0

--- a/solution.py
+++ b/solution.py
@@ -62,7 +62,10 @@
     row_count = per_group * seq_len
     weight = lm_head[0]
     gain = norm_gain[0]
-    whole = lax.all_gather(hidden, TENSOR, axis=3, tiled=True)
+    size = lax.axis_size(TENSOR)
+    parts = jnp.stack([hidden for _ in range(size)])
+    parts = lax.all_to_all(parts, TENSOR, split_axis=0, concat_axis=0)
+    whole = jnp.concatenate(parts, axis=3)
     flat = whole.reshape(row_count, full_width).astype(jnp.float32)
     mean_sq = jnp.mean(flat * flat, axis=1, keepdims=True)
     normed = (flat * lax.rsqrt(mean_sq + rms_epsilon) * gain).astype(jnp.bfloat16)

time: 220 us -> 406 us (1.85)
  waiting for transfers between devices: 110 us -> 244 us
  blocking collectives: 38.4 us -> 67.3 us
  starting transfers between devices: 17.4 us -> 34.7 us
  between operations: 14.9 us -> 1.48 us
  other arithmetic: 10.9 us -> 19.3 us
  local copies, waits for them, and re-layouts: 20.9 us -> 27.1 us
    all_to_all x0 -> x1, waiting for transfers between devices: none -> 240 us  [shards(): parts = lax.all_to_all(parts, TENSOR, split_axis=0, concat_axis=0)]
    all_gather x1 -> x0, waiting for transfers between devices: 106 us -> none  [shards(): whole = lax.all_gather(hidden, TENSOR, axis=3, tiled=True)]
    all_gather x2, blocking collectives: 38.4 us -> 67.3 us  [gathered_once(): both, at, found = (lax.all_gather(jnp.concatenate(lines), axis), 0, {})]
    all_to_all x0 -> x1, starting transfers between devices: none -> 17.5 us  [shards(): parts = lax.all_to_all(parts, TENSOR, split_axis=0, concat_axis=0)]
    convert_element_type x0 -> x1, local copies, waits for them, and re-layouts: none -> 14.5 us  [shards(): (flat * lax.rsqrt(mean_sq + rms_epsilon) * gain).astype(jnp.bfloat16)]
    all_gather x1 -> x0, local copies, waits for them, and re-layouts: 11.8 us -> none  [shards(): whole = lax.all_gather(hidden, TENSOR, axis=3, tiled=True)]
    convert_element_type x1, other arithmetic: 1.53 us -> 7.94 us  [shards(): (flat * lax.rsqrt(mean_sq + rms_epsilon) * gain).astype(jnp.bfloat16)]
    another operation x0 -> x2, local copies, waits for them, and re-layouts: none -> 6.19 us  [the longest x1 5.23 us: shards(): parts = jnp.stack([hidden for _ in range(size)])]
  transfers between devices with their start and end apart: 2 -> 2, of which waited for: 2 -> 2; matrix products, arithmetic and copies ran while one was open for 1% -> 0% of each run, Pallas kernels for 0% -> 0%
where the time goes in v1:
time: 406 us; the launch traced here: 405 us
  waiting for transfers between devices  244 us (60%)
  blocking collectives  67.3 us (17%)
  starting transfers between devices  34.7 us (9%)
  local copies, waits for them, and re-layouts  27.1 us (7%)
  other arithmetic  19.3 us (5%)
  matrix products  10.6 us (3%)
    all_to_all x1, waiting for transfers between devices, shards(): parts = lax.all_to_all(parts, TENSOR, split_axis=0, concat_axis=0)  240 us
    all_gather x2, blocking collectives, gathered_once(): both, at, found = (lax.all_gather(jnp.concatenate(lines), axis), 0, {})  67.3 us
    all_to_all x1, starting transfers between devices, shards(): parts = lax.all_to_all(parts, TENSOR, split_axis=0, concat_axis=0)  17.5 us
    all_to_all x1, starting transfers between devices, from_everyone(): lax.all_to_all(jnp.broadcast_to(x[None], (peers, *x.shape)), axis, 0, 0,...  17.1 us
    convert_element_type x1, local copies, waits for them, and re-layouts, shards(): (flat * lax.rsqrt(mean_sq + rms_epsilon) * gain).astype(jnp.bfloat16)  14.5 us
    dot_general x1, matrix products, shards(): logits = jnp.dot(normed, weight, preferred_element_type=jnp.float32)  10.6 us
  transfers between devices with their start and end apart: 2, of which 2 were waited for; matrix products, arithmetic and copies ran while one was open for 0% of the time, Pallas kernels for 0%

profile of v1, /device:TPU:1, one launch (start us, length us, event | category | flops | bytes accessed | tf_op | source)
XLA Modules:
  0.0 404.9 jit_solution(5032539184284307139)
XLA Ops:
  0.6 1.0 copy.12
  1.6 5.2 %stack.2 = bf16[64,1,16,96,32]{3,2,4,1,0:T(8,128)(2,1)} broadcast(bf16[16,96,32]{1,0,2:T(8,128)(2,1)S(1)} %copy.12), dimensions={2,3,4} | broadcast | bytes 6389760 | tf_op jit(solution)/shard_map/stack | solution.py:66
  6.8 17.5 %all-to-all-start = ((bf16[64,1,16,96,32]{3,2,4,1,0:T(8,128)(2,1)}), bf16[64,1,16,96,32]{3,2,4,1,0:T(8,128)(2,1)}, u32[]{:S(2)}, u32[]{:S(2)}) async-start(bf16[64,1,16,96,32]{3,2,4,1,0:T(8,128)(2,1)} %stack.2), calls=%async_computation | async-start | bytes 16777216 | tf_op jit(solution)/shard_map/all_to_all | solution.py:67
  24.4 0.5 broadcast.191
  24.9 0.7 reduce.102
  25.6 0.1 eq.16
  25.7 240.5 %all-to-all-done = bf16[64,1,16,96,32]{3,2,4,1,0:T(8,128)(2,1)} async-done(((bf16[64,1,16,96,32]{3,2,4,1,0:T(8,128)(2,1)}), bf16[64,1,16,96,32]{3,2,4,1,0:T(8,128)(2,1)}, u32[]{:S(2)}, u32[]{:S(2)}) %all-to-all-start) | async-done | bytes 6291488 | tf_op jit(solution)/shard_map/all_to_all | solution.py:67
  266.2 5.6 %fusion = f32[16,96]{1,0:T(8,128)S(1)} fusion(bf16[64,1,16,96,32]{3,2,4,1,0:T(8,128)(2,1)} %all-to-all-done), kind=kLoop, calls=%fused_computation.2 | loop fusion | flops 9435648 | bytes 6297600 | tf_op jit(solution)/shard_map/reduce_sum | solution.py:70
  271.8 7.9 %fusion.3 = bf16[1,16,96,64,32]{2,1,4,0,3:T(8,128)(2,1)} fusion(bf16[64,1,16,96,32]{3,2,4,1,0:T(8,128)(2,1)} %all-to-all-done, f32[64,32]{1,0:T(8,128)S(1)} %mul.1594, f32[16,96]{1,0:T(8,128)S(1)} %add_rsqrt_fusion), kind=kLoop, calls=%fused_computation.5 | loop fusion | flops 12582912 | bytes 12597248 | tf_op jit(solution)/shard_map/convert_element_type | solution.py:71
  279.7 14.5 %convert_element_type.21 = bf16[1536,2048]{0,1:T(8,128)(2,1)} reshape(bf16[1,16,96,64,32]{2,1,4,0,3:T(8,128)(2,1)} %fusion.3) | data formatting | bytes 12582912 | tf_op jit(solution)/shard_map/convert_element_type | solution.py:71
  294.3 10.6 %fusion.104 = (f32[1536]{0:T(1024)S(1)}, f32[1536,1024]{0,1:T(8,128)S(1)}) fusion(bf16[1536,2048]{0,1:T(8,128)(2,1)} %convert_element_type.21, bf16[1,2048,1024]{2,1,0:T(8,128)(2,1)} %param.7), kind=kOutput, calls=%fused_computation.252 | convolution fusion | flops 6444022272 | bytes 16783360 | tf_op jit(solution)/shard_map/dot_general | solution.py:72
  304.9 2.3 fusion.4
  307.3 34.4 %all-gather.2 = f32[8,4,1536]{2,1,0:T(4,128)S(1)} all-gather(f32[1,4,1536]{2,1,0:T(4,128)S(1)} %maximum_bitcast_fusion), channel_id=2, replica_groups=mesh['seed'=2,'dp'=4,'tensor_0'=8,'tensor_1'=8] {'tensor_0'}, dimensions={0}, use_global_device_ids=true | all-gather | bytes 221184 | tf_op jit(solution)/shard_map/all_gather | solution.py:19
  341.8 0.1 fusion.72
  341.9 0.2 fusion.49
  342.1 0.1 fusion.51
  342.3 32.9 %all-gather.3 = f32[8,4,1536]{2,1,0:T(4,128)S(1)} all-gather(f32[1,4,1536]{2,1,0:T(4,128)S(1)} %maximum_bitcast_fusion.1), channel_id=3, replica_groups=mesh['seed'=2,'dp'=4,'tensor_0'=8,'tensor_1'=8] {'tensor_1'}, dimensions={0}, use_global_device_ids=true | all-gather | bytes 221184 | tf_op jit(solution)/shard_map/all_gather | solution.py:19
  375.2 0.3 slice_reduce_fusion.30
  375.5 0.2 slice_reduce_fusion.31
  375.7 0.1 squeeze.325
  378.7 0.1 squeeze.294
  378.7 0.1 squeeze.327
  378.8 0.1 squeeze.295
  378.9 0.1 squeeze.328
  380.3 0.2 select_reduce_fusion.1
  380.6 0.1 divide_dynamic-update-slice_fusion
  380.7 0.6 broadcast_in_dim.8
  381.3 17.1 %all-to-all-start.1 = ((f32[8,1,64]{2,1,0:T(1,128)}), f32[8,1,64]{2,1,0:T(1,128)S(1)}, u32[]{:S(2)}, u32[]{:S(2)}) async-start(f32[8,1,64]{2,1,0:T(1,128)} %broadcast_in_dim.8), calls=%async_computation.1 | async-start | bytes 8192 | tf_op jit(solution)/shard_map/all_to_all | solution.py:39
  398.4 0.7 sqrt_select_fusion
  399.1 3.9 all-to-all-done.1
  403.1 0.6 broadcast_multiply_fusion
  404.3 0.6 broadcast_subtract_fusion
  (76 shorter events, 4.4 us)
Async XLA Ops:
  6.8 18.1 %copy-start = (f32[1,2048]{1,0:T(1,128)S(1)}, f32[1,2048]{1,0:T(1,128)}, u32[]{:S(2)}) copy-start(f32[1,2048]{1,0:T(1,128)} %param.6) | copy-start | bytes 24580
  6.8 18.8 %copy-start.1 = (s32[16,96]{1,0:T(8,128)S(1)}, s32[16,96]{1,0:T(8,128)}, u32[]{:S(2)}) copy-start(s32[16,96]{1,0:T(8,128)} %param.8) | copy-start | bytes 18436
  6.8 259.3 %all-to-all-start = ((bf16[64,1,16,96,32]{3,2,4,1,0:T(8,128)(2,1)}), bf16[64,1,16,96,32]{3,2,4,1,0:T(8,128)(2,1)}, u32[]{:S(2)}, u32[]{:S(2)}) async-start(bf16[64,1,16,96,32]{3,2,4,1,0:T(8,128)(2,1)} %stack.2), calls=%async_computation | async-start | bytes 16777216 | tf_op jit(solution)/shard_map/all_to_all | solution.py:67
  304.9 75.5 %copy-start.2 = (s32[16]{0:T(128)S(1)}, s32[16]{0:T(128)}, u32[]{:S(2)}) copy-start(s32[16]{0:T(128)} %param.9) | copy-start | bytes 196
  381.3 21.7 %all-to-all-start.1 = ((f32[8,1,64]{2,1,0:T(1,128)}), f32[8,1,64]{2,1,0:T(1,128)S(1)}, u32[]{:S(2)}, u32[]{:S(2)}) async-start(f32[8,1,64]{2,1,0:T(1,128)} %broadcast_in_dim.8), calls=%async_computation.1 | async-start | bytes 8192 | tf_op jit(solution)/shard_map/all_to_all | solution.py:39
